TPU v7x, 32 devices: a whole 2x2x4 slice. The times are simulated.
32 devices in a mesh: rows: 32 (over z, y, x, core).
Axes of the slice: x: 2, y: 2, z: 4, core: 2. Of those that a mesh axis runs over, the one named last changes fastest.
Arguments:
- snapshots: float32 [16384, 512], P('rows'), may hold values from -100 to 100
- validation: float32 [16384, 512], P('rows'), may hold values from -100 to 100
- eigenvectors: float32 [512, 64], replicated, may hold values from -0.25 to 0.25
- eigenvalues: float32 [64], replicated, may hold values from 16 to 256
Outputs:
- gram: float32 [512, 512], replicated
- modes: float32 [64, 16384], P(None, 'rows')
- train_coef: float32 [64, 512], replicated
- valid_coef: float32 [64, 512], replicated
All inputs are finite; a program needn't handle non-finite values.
Results may differ from a plain program's by a relative error of at most 0.000071.
Values sent between devices are 32-bit elements; how exact they have to be, the bound alone decides.
No kernel may reach another device: no remote copies, remote signals or barrier semaphores. Data moves between devices by JAX's collectives and lax.ppermute only.
A program may use at most 64 MiB of HBM per device.

v0:
```python
import jax
import jax.numpy as jnp
from jax import lax
from jax.sharding import PartitionSpec as P


def body(snapshots, validation, eigenvectors, eigenvalues):
    highest = lax.Precision.HIGHEST
    devices = lax.axis_size("rows")
    total = snapshots.shape[0] * devices * 1.0
    gram_part = (
        lax.dot_general(
            snapshots,
            snapshots,
            (((0,), (0,)), ((), ())),
            precision=highest,
            preferred_element_type=jnp.float32,
        )
        / total
    )
    scales = lax.rsqrt(eigenvalues)
    modes = (
        lax.dot_general(
            eigenvectors,
            snapshots,
            (((0,), (1,)), ((), ())),
            precision=highest,
            preferred_element_type=jnp.float32,
        )
        * scales[:, None]
    )
    gram = lax.psum(gram_part, "rows")
    valid_part = (
        jnp.dot(modes, validation, precision=highest, preferred_element_type=jnp.float32) / total
    )
    valid_coef = lax.psum(valid_part, "rows")
    train_coef = (
        lax.dot_general(
            eigenvectors,
            gram,
            (((0,), (0,)), ((), ())),
            precision=highest,
            preferred_element_type=jnp.float32,
        )
        * scales[:, None]
    )
    return (gram, modes, train_coef, valid_coef)


def solution(mesh):
    in_specs = (P("rows", None), P("rows", None), P(), P())
    out_specs = (P(), P(None, "rows"), P(), P())
    return jax.shard_map(body, mesh=mesh, in_specs=in_specs, out_specs=out_specs, check_vma=False)
```

profile of v0, /device:TPU:0, one launch (start us, length us, event | category | flops | bytes accessed | tf_op | source)
XLA Modules:
  0.0 159.9 jit_solution(1666710015621987377)
XLA Ops:
  7.2 0.0 copy-start
  7.2 0.0 all-reduce.3.cloned.1.call-start
  7.2 0.7 rsqrt.3
  8.0 0.4 copy-done
  8.4 0.0 copy-start.3
  8.4 2.8 %convolution_multiply_fusion = f32[512,512]{1,0:T(8,128)} fusion(f32[512,512]{1,0:T(8,128)S(1)} %copy-done), kind=kOutput, calls=%fused_computation | convolution fusion | flops 1610874880 | bytes 2097152 | tf_op jit(solution)/shard_map/dot_general | solution.py:12
  11.2 0.0 copy-done.3
  11.2 0.0 copy-start.2
  11.2 1.1 convolution_multiply_fusion.3
  12.4 0.1 copy-done.2
  12.5 0.0 copy-start.4
  12.5 1.4 convolution_multiply_fusion.1
  13.9 0.0 copy-done.4
  13.9 0.0 all-reduce.3.cloned.1.call-update
  13.9 134.7 %all-reduce.3.cloned.1.call-done = (f32[512,512]{1,0:T(8,128)}, f32[64,512]{1,0:T(8,128)}) async-done(((f32[512,512]{1,0:T(8,128)}, f32[64,512]{1,0:T(8,128)}), (f32[512,512]{1,0:T(8,128)}, f32[64,512]{1,0:T(8,128)})) %all-reduce.3.cloned.1.call-update) | async-done | bytes 1179664 | tf_op jit(solution)/shard_map/psum | solution.py:32
  148.7 0.0 copy-start.1
  148.7 2.8 %fusion = f32[64,512]{1,0:T(8,128)} fusion(f32[512,512]{1,0:T(8,128)} %get-tuple-element.6, f32[512,64]{0,1:T(8,128)S(1)} %copy-done.3, f32[64]{0:T(128)S(1)} %rsqrt.3), kind=kOutput, calls=%fused_computation.3 | convolution fusion | flops 201359360 | bytes 1310976 | tf_op jit(solution)/shard_map/dot_general | solution.py:38
  151.4 0.0 copy-done.1
  151.4 0.0 copy-start.5
  151.4 1.0 copy.10
  152.4 0.1 copy-done.5
  152.4 0.7 copy.11
Async XLA Ops:
  7.2 1.2 copy-start
  7.2 141.5 %all-reduce.3.cloned.1.call-start = ((), (), s32[]{:S(2)}) async-start(), calls=%async_computation | async-start | bytes 2359296 | tf_op jit(solution)/shard_map/psum | solution.py:32
  8.4 2.8 %copy-start.3 = (f32[512,64]{0,1:T(8,128)S(1)}, f32[512,64]{0,1:T(8,128)}, u32[]{:S(2)}) copy-start(f32[512,64]{0,1:T(8,128)} %param.6) | copy-start | bytes 393220
  11.2 1.2 copy-start.2
  12.5 1.4 copy-start.4
  148.7 2.8 %copy-start.1 = (f32[512,512]{1,0:T(8,128)S(1)}, f32[512,512]{1,0:T(8,128)}, u32[]{:S(2)}) copy-start(f32[512,512]{1,0:T(8,128)} %get-tuple-element.6) | copy-start | bytes 3145732
  151.4 1.0 copy-start.5
Sparse Core Ops, SparseCore 0:
  14.0 134.5 all-reduce.2
where the time goes:
time: 160 us
  waiting for transfers between devices  135 us (84%)
  between operations  14 us (9%)
  matrix products  8.12 us (5%)
  local copies, waits for them, and re-layouts  2.99 us (2%)
    psum x1, waiting for transfers between devices, body(): gram = lax.psum(gram_part, 'rows')  135 us
  transfers between devices with their start and end apart: 1, of which 1 were waited for; matrix products, arithmetic and copies ran while one was open for 0% of the time, Pallas kernels for 0%

commit v1 on v0

--- a/solution.py
+++ b/solution.py
@@ -29,7 +29,9 @@
         )
         * scales[:, None]
     )
-    gram = lax.psum(gram_part, "rows")
+    gram = gram_part
+    for hop in (1, 2, 4, 8, 16):
+        gram = gram + lax.ppermute(gram, "rows", [(dev, dev ^ hop) for dev in range(32)])
     valid_part = (
         jnp.dot(modes, validation, precision=highest, preferred_element_type=jnp.float32) / total
     )

time: 160 us -> 243 us (1.52)
  waiting for transfers between devices: 135 us -> 209 us
  starting transfers between devices: 0.04 us -> 9.3 us
    ppermute x0 -> x5, waiting for transfers between devices: none -> 113 us  [body(): lax.ppermute(gram, 'rows', [(dev, dev ^ hop) for dev in range(32)])]
    psum x1, waiting for transfers between devices: 135 us -> 95.8 us  [body(): valid_coef = lax.psum(valid_part, 'rows')]
    ppermute x0 -> x5, starting transfers between devices: none -> 9.26 us  [body(): lax.ppermute(gram, 'rows', [(dev, dev ^ hop) for dev in range(32)])]
  transfers between devices with their start and end apart: 1 -> 6, of which waited for: 1 -> 6; matrix products, arithmetic and copies ran while one was open for 0% -> 2% of each run, Pallas kernels for 0% -> 0%
where the time goes in v1:
time: 243 us
  waiting for transfers between devices  209 us (86%)
  between operations  14.1 us (6%)
  starting transfers between devices  9.3 us (4%)
  matrix products  5.85 us (2%)
  local copies, waits for them, and re-layouts  2.78 us (1%)
    ppermute x5, waiting for transfers between devices, body(): lax.ppermute(gram, 'rows', [(dev, dev ^ hop) for dev in range(32)])  113 us
    psum x1, waiting for transfers between devices, body(): valid_coef = lax.psum(valid_part, 'rows')  95.8 us
    ppermute x5, starting transfers between devices, body(): lax.ppermute(gram, 'rows', [(dev, dev ^ hop) for dev in range(32)])  9.26 us
  transfers between devices with their start and end apart: 6, of which 6 were waited for; matrix products, arithmetic and copies ran while one was open for 2% of the time, Pallas kernels for 0%

profile of v1, /device:TPU:0, one launch (start us, length us, event | category | flops | bytes accessed | tf_op | source)
XLA Modules:
  0.0 243.1 jit_solution(3521056402145835043)
XLA Ops:
  7.2 0.0 copy-start
  7.2 0.0 all-reduce.2.cloned.1.call-start
  7.2 1.2 copy-done
  8.4 1.9 convolution_multiply_fusion
  10.3 0.6 collective-permute-start
  10.8 2.3 collective-permute-done
  13.1 0.2 add.17
  13.3 2.9 %collective-permute-start.1 = (f32[512,512]{1,0:T(8,128)S(1)}, f32[512,512]{1,0:T(8,128)S(1)}, u32[]{:S(2)}, u32[]{:S(2)}) collective-permute-start(f32[512,512]{1,0:T(8,128)S(1)} %add.17), channel_id=1, source_target_pairs={{0,2},{1,3},{2,0},{3,1},{4,6},{5,7},{6,4},{7,5},{8,10},{9,11},{10,... | collective-permute-start | bytes 3145736 | tf_op jit(solution)/shard_map/ppermute | solution.py:34
  16.2 23.5 %collective-permute-done.1 = f32[512,512]{1,0:T(8,128)S(1)} collective-permute-done((f32[512,512]{1,0:T(8,128)S(1)}, f32[512,512]{1,0:T(8,128)S(1)}, u32[]{:S(2)}, u32[]{:S(2)}) %collective-permute-start.1) | collective-permute-done | bytes 1048608 | tf_op jit(solution)/shard_map/ppermute | solution.py:34
  39.7 0.2 add.18
  39.9 1.8 collective-permute-start.2
  41.7 22.9 %collective-permute-done.2 = f32[512,512]{1,0:T(8,128)S(1)} collective-permute-done((f32[512,512]{1,0:T(8,128)S(1)}, f32[512,512]{1,0:T(8,128)S(1)}, u32[]{:S(2)}, u32[]{:S(2)}) %collective-permute-start.2) | collective-permute-done | bytes 1048608 | tf_op jit(solution)/shard_map/ppermute | solution.py:34
  64.6 0.2 add.19
  64.8 0.0 copy-start.5
  64.8 0.0 copy-start.3
  64.8 1.6 collective-permute-start.3
  66.4 22.2 %collective-permute-done.3 = f32[512,512]{1,0:T(8,128)S(1)} collective-permute-done((f32[512,512]{1,0:T(8,128)S(1)}, f32[512,512]{1,0:T(8,128)S(1)}, u32[]{:S(2)}, u32[]{:S(2)}) %collective-permute-start.3) | collective-permute-done | bytes 1048608 | tf_op jit(solution)/shard_map/ppermute | solution.py:34
  88.7 0.2 add.20
  88.9 0.0 copy-start.2
  88.9 2.3 collective-permute-start.4
  91.2 0.0 copy-done.5
  91.2 0.0 copy-done.3
  91.2 1.1 convolution_multiply_fusion.3
  92.4 0.0 copy-done.2
  92.4 0.0 copy-start.4
  92.4 1.4 convolution_multiply_fusion.1
  93.8 0.0 copy-done.4
  93.8 0.0 all-reduce.2.cloned.1.call-update
  93.8 42.1 %collective-permute-done.4 = f32[512,512]{1,0:T(8,128)} collective-permute-done((f32[512,512]{1,0:T(8,128)S(1)}, f32[512,512]{1,0:T(8,128)}, u32[]{:S(2)}, u32[]{:S(2)}) %collective-permute-start.4) | collective-permute-done | bytes 1048608 | tf_op jit(solution)/shard_map/ppermute | solution.py:34
  136.0 1.4 add.21
  137.4 0.0 copy-start.1
  137.4 1.4 fusion
  138.8 95.8 %all-reduce.2.cloned.1.call-done = f32[64,512]{1,0:T(8,128)} async-done(((f32[64,512]{1,0:T(8,128)}), f32[64,512]{1,0:T(8,128)}) %all-reduce.2.cloned.1.call-update) | async-done | bytes 131088 | tf_op jit(solution)/shard_map/psum | solution.py:38
  234.7 1.6 copy.9
  236.2 0.0 copy-done.1
  (1 shorter events, 0.0 us)
Async XLA Ops:
  7.2 1.2 copy-start
  7.2 227.5 %all-reduce.2.cloned.1.call-start = ((), (), s32[]{:S(2)}) async-start(), calls=%async_computation | async-start | bytes 262144 | tf_op jit(solution)/shard_map/psum | solution.py:38
  10.3 2.8 %collective-permute-start = (f32[512,512]{1,0:T(8,128)S(1)}, f32[512,512]{1,0:T(8,128)S(1)}, u32[]{:S(2)}, u32[]{:S(2)}) collective-permute-start(f32[512,512]{1,0:T(8,128)S(1)} %convolution_multiply_fusion), channel_id=1, source_target_pairs={{0,1},{1,0},{2,3},{3,2},{4,5},{5,4},{6,7},{7,6},{8,9},{9,8},{10,11... | collective-permute-start | bytes 3145736 | tf_op jit(solution)/shard_map/ppermute | solution.py:34
  13.3 26.4 %collective-permute-start.1 = (f32[512,512]{1,0:T(8,128)S(1)}, f32[512,512]{1,0:T(8,128)S(1)}, u32[]{:S(2)}, u32[]{:S(2)}) collective-permute-start(f32[512,512]{1,0:T(8,128)S(1)} %add.17), channel_id=1, source_target_pairs={{0,2},{1,3},{2,0},{3,1},{4,6},{5,7},{6,4},{7,5},{8,10},{9,11},{10,... | collective-permute-start | bytes 3145736 | tf_op jit(solution)/shard_map/ppermute | solution.py:34
  39.9 24.7 %collective-permute-start.2 = (f32[512,512]{1,0:T(8,128)S(1)}, f32[512,512]{1,0:T(8,128)S(1)}, u32[]{:S(2)}, u32[]{:S(2)}) collective-permute-start(f32[512,512]{1,0:T(8,128)S(1)} %add.18), channel_id=1, source_target_pairs={{0,4},{1,5},{2,6},{3,7},{4,0},{5,1},{6,2},{7,3},{8,12},{9,13},{10,... | collective-permute-start | bytes 3145736 | tf_op jit(solution)/shard_map/ppermute | solution.py:34
  64.8 26.4 %copy-start.5 = (f32[64]{0:T(128)S(1)}, f32[64]{0:T(128)}, u32[]{:S(2)}) copy-start(f32[64]{0:T(128)} %param.7) | copy-start | bytes 772
  64.8 26.4 %copy-start.3 = (f32[512,64]{0,1:T(8,128)S(1)}, f32[512,64]{0,1:T(8,128)}, u32[]{:S(2)}) copy-start(f32[512,64]{0,1:T(8,128)} %param.6) | copy-start | bytes 393220
  64.8 23.8 %collective-permute-start.3 = (f32[512,512]{1,0:T(8,128)S(1)}, f32[512,512]{1,0:T(8,128)S(1)}, u32[]{:S(2)}, u32[]{:S(2)}) collective-permute-start(f32[512,512]{1,0:T(8,128)S(1)} %add.19), channel_id=1, source_target_pairs={{0,8},{1,9},{2,10},{3,11},{4,12},{5,13},{6,14},{7,15},{8,0},{9,1},... | collective-permute-start | bytes 3145736 | tf_op jit(solution)/shard_map/ppermute | solution.py:34
  88.9 3.5 %copy-start.2 = (f32[512,512]{1,0:T(8,128)S(1)}, f32[512,512]{1,0:T(8,128)}, u32[]{:S(2)}) copy-start(f32[512,512]{1,0:T(8,128)} %param.5) | copy-start | bytes 3145732
  88.9 47.1 %collective-permute-start.4 = (f32[512,512]{1,0:T(8,128)S(1)}, f32[512,512]{1,0:T(8,128)}, u32[]{:S(2)}, u32[]{:S(2)}) collective-permute-start(f32[512,512]{1,0:T(8,128)S(1)} %add.20), channel_id=1, source_target_pairs={{0,16},{1,17},{2,18},{3,19},{4,20},{5,21},{6,22},{7,23},{8,24},{9,... | collective-permute-start | bytes 3145736 | tf_op jit(solution)/shard_map/ppermute | solution.py:34
  92.4 1.4 copy-start.4
  137.4 98.8 %copy-start.1 = (f32[512,512]{1,0:T(8,128)}, f32[512,512]{1,0:T(8,128)S(1)}, u32[]{:S(2)}) copy-start(f32[512,512]{1,0:T(8,128)S(1)} %add.21) | copy-start | bytes 3145732
Sparse Core Ops, SparseCore 0:
  93.9 140.6 all-reduce.1
